TPU v7x, 32 devices: a whole 2x2x4 slice. The times are simulated.
32 devices in a mesh: er: 2 (over x), ec: 4 (over z), dp: 4 (over y, core).
Axes of the slice: x: 2, y: 2, z: 4, core: 2. Of those that a mesh axis runs over, the one named last changes fastest.
Arguments:
- out_grad: bfloat16 [4, 512, 4096], P('dp', 'er', 'ec'), may hold values from -6 to 6
- route_probs: float32 [4, 512], P('dp', 'er'), may hold values from 0.1 to 1
- expert_ids: int32 [4, 512], P('dp', 'er'), may hold values from 0 to 1, as said below
- slot_ids: int32 [4, 512], P('dp', 'er'), may hold values from 0 to 143, as said below
- gate_pre: bfloat16 [4, 2, 288, 768], P('dp', 'er'), may hold values from -6 to 6
- up_act: bfloat16 [4, 2, 288, 768], P('dp', 'er'), may hold values from -6 to 6
- w_gate: bfloat16 [2, 4096, 768], P('er', 'ec'), may hold values from -0.09375 to 0.09375
- w_up: bfloat16 [2, 4096, 768], P('er', 'ec'), may hold values from -0.09375 to 0.09375
- w_down: bfloat16 [2, 768, 4096], P('er', None, 'ec'), may hold values from -0.21875 to 0.21875
Outputs:
- input_grad: bfloat16 [4, 512, 4096], P('dp', 'er', 'ec')
- down_grad: float32 [2, 768, 4096], P('er', 'dp', 'ec')
Inputs may be any that keep to these rules, and one draw needn't show every extreme that they name: `expert_ids`: within each group of 256 tokens no expert is chosen by more than 144 tokens; in every replica some expert is chosen by exactly 144 tokens of every group of that replica. `slot_ids`: tokens of one group that chose the same expert have distinct slots.
All inputs are finite; a program needn't handle non-finite values.
Results may differ from a plain program's by a relative error of at most 0.015.
Values may be sent and summed in bfloat16 or wider, within the bound.
No kernel may reach another device: no remote copies, remote signals or barrier semaphores. Data moves between devices by JAX's collectives and lax.ppermute only.
A program may use at most 64 MiB of HBM per device.

v0:
```python
import jax
import jax.numpy as jnp
from jax import lax
from jax.sharding import PartitionSpec as P


def swiglu_grads(hid_grad, pre_rows, up_rows):
    pre_float = pre_rows.astype(jnp.float32)
    up_float = up_rows.astype(jnp.float32)
    sigmoid = jax.nn.sigmoid(pre_float)
    gate_grad = (hid_grad * up_float * sigmoid * (1.0 + pre_float * (1.0 - sigmoid))).astype(
        jnp.bfloat16
    )
    up_grad = (hid_grad * pre_float * sigmoid).astype(jnp.bfloat16)
    return (gate_grad, up_grad)


def reduce_weights(hidden, arrived):
    replicas = lax.axis_size("dp")
    summed = lax.psum_scatter(
        lax.dot_general(
            hidden, arrived, (((0,), (0,)), ((), ())), preferred_element_type=jnp.float32
        ),
        "dp",
        scatter_dimension=0,
        tiled=True,
    )
    return summed / replicas


def body(out_grad, route_probs, expert_ids, slot_ids, gate_pre, up_act, w_gate, w_up, w_down):
    tokens = out_grad[0]
    experts = lax.axis_size("er")
    capacity = gate_pre.shape[2] // experts
    slot_count = experts * capacity
    position = expert_ids[0] * capacity + slot_ids[0]
    scaled = (route_probs[0][:, None] * tokens.astype(jnp.float32)).astype(jnp.bfloat16)
    source = (
        jnp.zeros((slot_count,), jnp.int32)
        .at[position]
        .set(jnp.arange(tokens.shape[0], dtype=jnp.int32))
    )
    filled = jnp.zeros((slot_count,), jnp.bool_).at[position].set(True)
    outgoing = jnp.where(filled[:, None], scaled[source], jnp.zeros((), jnp.bfloat16))
    arrived = lax.all_to_all(outgoing, "er", split_axis=0, concat_axis=0, tiled=True)
    pre_rows = gate_pre[0, 0]
    up_rows = up_act[0, 0]
    pre_float = pre_rows.astype(jnp.float32)
    hidden = (pre_float * jax.nn.sigmoid(pre_float) * up_rows.astype(jnp.float32)).astype(
        jnp.bfloat16
    )
    partial_value = lax.dot_general(
        arrived, w_down[0], (((1,), (1,)), ((), ())), preferred_element_type=jnp.float32
    )
    hid_grad = lax.psum(partial_value.astype(jnp.bfloat16), "ec").astype(jnp.float32)
    gate_grad, up_grad = swiglu_grads(hid_grad, pre_rows, up_rows)
    slot_grad = (
        lax.dot_general(
            gate_grad, w_gate[0], (((1,), (1,)), ((), ())), preferred_element_type=jnp.float32
        )
        + lax.dot_general(
            up_grad, w_up[0], (((1,), (1,)), ((), ())), preferred_element_type=jnp.float32
        )
    ).astype(jnp.bfloat16)
    returned = lax.all_to_all(slot_grad, "er", split_axis=0, concat_axis=0, tiled=True)
    down_part = reduce_weights(hidden, arrived)
    input_grad = returned[position]
    return (input_grad[None], down_part[None])


def solution(mesh):
    in_specs = (
        P("dp", "er", "ec"),
        P("dp", "er"),
        P("dp", "er"),
        P("dp", "er"),
        P("dp", "er", None, None),
        P("dp", "er", None, None),
        P("er", "ec", None),
        P("er", "ec", None),
        P("er", None, "ec"),
    )
    out_specs = (P("dp", "er", "ec"), P("er", "dp", "ec"))
    return jax.shard_map(body, mesh=mesh, in_specs=in_specs, out_specs=out_specs, check_vma=False)
```

profile of v0, /device:TPU:0, one launch (start us, length us, event | category | flops | bytes accessed | tf_op | source)
XLA Modules:
  0.0 94.2 jit_solution(13919401980403054712)
XLA Ops:
  8.0 0.0 copy-start
  8.0 0.0 all-reduce.2.cloned.1.call-start
  8.1 0.8 compare_select_fusion
  8.9 1.5 %scatter_custom_fusion = pred[288]{0:T(512)(128)(4,1)S(1)} fusion(s32[256]{0:T(256)S(1)} %bitcast.74, pred[256]{0:T(512)(128)(4,1)S(1)} %broadcast.48, pred[]{:T(512)} %constant.9.clone.1), kind=kCustom, calls=%fused_computation.49 | custom fusion | bytes 289 | tf_op jit(solution)/shard_map/scatter | solution.py:43
  10.4 0.1 broadcast_in_dim.35
  10.5 1.4 %scatter_custom_fusion.1 = s32[288]{0:T(512)S(1)} fusion(s32[256]{0:T(256)S(1)} %bitcast.75, s32[256]{0:T(256)S(1)} %iota.3, s32[]{:T(128)} %constant.2.clone.1), kind=kCustom, calls=%fused_computation.47 | custom fusion | bytes 1156 | tf_op jit(solution)/shard_map/scatter | solution.py:41
  11.9 1.2 %fusion.18 = bf16[256,1024]{1,0:T(8,128)(2,1)S(1)} fusion(bf16[1,256,1024]{2,1,0:T(8,128)(2,1)} %param.9, f32[256]{0:T(256)} %bitcast.77), kind=kLoop, calls=%fused_computation.23 | loop fusion | flops 786432 | bytes 1049600 | tf_op jit(solution)/shard_map/convert_element_type | solution.py:37
  13.1 2.1 %gather_fusion = bf16[288,1024]{1,0:T(8,128)(2,1)S(1)} fusion(bf16[256,1024]{1,0:T(8,128)(2,1)S(1)} %fusion.18, s32[1024]{0:T(1024)S(1)} %pad_clamp_fusion.1), kind=kCustom, calls=%fused_computation | custom fusion | bytes 1180800 | tf_op jit(solution)/shard_map/gather | solution.py:44
  15.2 0.0 copy-start.1
  15.2 0.1 broadcast_select_fusion
  15.3 12.8 %all_to_all.21 = bf16[2,144,1024]{2,1,0:T(8,128)(2,1)S(1)} all-to-all(bf16[2,144,1024]{2,1,0:T(8,128)(2,1)S(1)} %broadcast_select_fusion), channel_id=1, replica_groups=mesh['er'=2,'ec'=4,'dp'=4] {'er'}, dimensions={0} | all-to-all | bytes 1179648 | tf_op jit(solution)/shard_map/all_to_all | solution.py:45
  28.1 0.0 copy-done.1
  28.1 0.0 copy-start.3
  28.1 0.0 copy-start.4
  28.2 1.5 %fusion.15 = bf16[288,768]{1,0:T(8,128)(2,1)} fusion(bf16[288,1024]{1,0:T(8,128)(2,1)S(1)} %bitcast.71, bf16[1,768,1024]{2,1,0:T(8,128)(2,1)S(1)} %copy-done.1), kind=kOutput, calls=%fused_computation.18 | convolution fusion | flops 453206016 | bytes 2605056 | tf_op jit(solution)/shard_map/dot_general | solution.py:52
  29.6 0.0 all-reduce.2.cloned.1.call-update
  29.6 0.0 reduce-scatter.2.cloned.1.call-start
  29.7 0.0 copy-done.3
  29.7 0.0 copy-done.4
  29.7 2.7 %fusion.34 = f32[768,1024]{1,0:T(8,128)} fusion(bf16[288,1024]{1,0:T(8,128)(2,1)S(1)} %bitcast.72, bf16[1,1,288,768]{3,2,1,0:T(8,128)(2,1)S(1)} %copy-done.4, bf16[1,1,288,768]{3,2,1,0:T(8,128)(2,1)S(1)} %copy-done.3), kind=kOutput, calls=%fused_computation.39 | convolution fusion | flops 454754304 | bytes 4620288 | tf_op jit(solution)/shard_map/dot_general | solution.py:21
  32.4 0.0 reduce-scatter.2.cloned.1.call-update
  32.5 35.2 %all-reduce.2.cloned.1.call-done = bf16[288,768]{1,0:T(8,128)(2,1)} async-done(((bf16[288,768]{1,0:T(8,128)(2,1)}), bf16[288,768]{1,0:T(8,128)(2,1)}) %all-reduce.2.cloned.1.call-update) | async-done | bytes 442384 | tf_op jit(solution)/shard_map/psum | solution.py:55
  67.7 0.0 copy-done
  67.7 0.0 copy-start.2
  67.7 0.0 copy-start.5
  67.7 1.8 %fusion = f32[288,1024]{1,0:T(8,128)S(1)} fusion(bf16[1,1024,768]{2,1,0:T(8,128)(2,1)S(1)} %copy-done, bf16[1,1,288,768]{3,2,1,0:T(8,128)(2,1)S(1)} %copy-done.3, bf16[288,768]{1,0:T(8,128)(2,1)} %all-reduce.2.cloned.1.call-done), kind=kOutput, calls=%fused_computation.4 | convolution fusion | flops 454754304 | bytes 3637248 | tf_op jit(solution)/shard_map/dot_general | solution.py:61
  69.6 0.0 copy-done.2
  69.6 0.0 copy-done.5
  69.6 1.7 %fusion.12 = bf16[288,1024]{1,0:T(8,128)(2,1)} fusion(f32[288,1024]{1,0:T(8,128)S(1)} %fusion, bf16[1,1024,768]{2,1,0:T(8,128)(2,1)S(1)} %copy-done.2, bf16[288,768]{1,0:T(8,128)(2,1)S(1)} %copy-done.5, bf16[1,1,288,768]{3,2,1,0:T(8,128)(2,1)S(1)} %copy-done.4, bf16[1,1,288,768]{3,2,1,0:T(8,128)(2,1)S(1)} %copy-done.3), kind=kOutput, calls=%fused_computation.17 | convolution fusion | flops 456450048 | bytes 4669440 | tf_op jit(solution)/shard_map/dot_general | solution.py:58
  71.2 3.5 %all-to-all-start.1 = ((bf16[2,144,1024]{2,1,0:T(8,128)(2,1)}), bf16[2,144,1024]{2,1,0:T(8,128)(2,1)S(1)}, u32[]{:S(2)}, u32[]{:S(2)}) async-start(bf16[2,144,1024]{2,1,0:T(8,128)(2,1)} %bitcast.11), calls=%async_computation.1 | async-start | bytes 1179648 | tf_op jit(solution)/shard_map/all_to_all | solution.py:65
  74.8 8.0 %all-to-all-done.1 = bf16[2,144,1024]{2,1,0:T(8,128)(2,1)S(1)} async-done(((bf16[2,144,1024]{2,1,0:T(8,128)(2,1)}), bf16[2,144,1024]{2,1,0:T(8,128)(2,1)S(1)}, u32[]{:S(2)}, u32[]{:S(2)}) %all-to-all-start.1) | async-done | bytes 589856 | tf_op jit(solution)/shard_map/all_to_all | solution.py:65
  82.7 2.0 %gather_fusion.1 = bf16[256,1024]{1,0:T(8,128)(2,1)} fusion(bf16[288,1024]{1,0:T(8,128)(2,1)S(1)} %bitcast.69, s32[1024]{0:T(1024)S(1)} %pad_clamp_fusion), kind=kCustom, calls=%fused_computation.1 | custom fusion | bytes 1049600 | tf_op jit(solution)/shard_map/gather | solution.py:67
  84.7 0.0 reduce-scatter.2.cloned.1.call-done
  84.7 2.1 %multiply_bitcast_fusion = f32[1,192,1024]{2,1,0:T(8,128)} fusion(f32[192,1024]{1,0:T(8,128)} %reduce-scatter.2.cloned.1.call-done), kind=kLoop, calls=%fused_computation.37 | loop fusion | flops 196608 | bytes 1572864 | tf_op jit(solution)/shard_map/broadcast_in_dim | solution.py:68
  (5 shorter events, 0.0 us)
Async XLA Ops:
  8.0 59.7 %copy-start = (bf16[1,1024,768]{2,1,0:T(8,128)(2,1)S(1)}, bf16[1,1024,768]{2,1,0:T(8,128)(2,1)}, u32[]{:S(2)}) copy-start(bf16[1,1024,768]{2,1,0:T(8,128)(2,1)} %param.16) | copy-start | bytes 4718596
  8.0 59.7 %all-reduce.2.cloned.1.call-start = ((), (), s32[]{:S(2)}) async-start(), calls=%async_computation.3 | async-start | bytes 884736 | tf_op jit(solution)/shard_map/psum | solution.py:55
  15.2 13.0 %copy-start.1 = (bf16[1,768,1024]{2,1,0:T(8,128)(2,1)S(1)}, bf16[1,768,1024]{2,1,0:T(8,128)(2,1)}, u32[]{:S(2)}) copy-start(bf16[1,768,1024]{2,1,0:T(8,128)(2,1)} %param.17) | copy-start | bytes 4718596
  28.1 1.5 %copy-start.3 = (bf16[1,1,288,768]{3,2,1,0:T(8,128)(2,1)S(1)}, bf16[1,1,288,768]{3,2,1,0:T(8,128)(2,1)}, u32[]{:S(2)}) copy-start(bf16[1,1,288,768]{3,2,1,0:T(8,128)(2,1)} %param.13) | copy-start | bytes 1327108
  28.1 1.5 %copy-start.4 = (bf16[1,1,288,768]{3,2,1,0:T(8,128)(2,1)S(1)}, bf16[1,1,288,768]{3,2,1,0:T(8,128)(2,1)}, u32[]{:S(2)}) copy-start(bf16[1,1,288,768]{3,2,1,0:T(8,128)(2,1)} %param.14) | copy-start | bytes 1327108
  29.6 55.0 %reduce-scatter.2.cloned.1.call-start = ((), (), s32[]{:S(2)}) async-start(), calls=%async_computation.4 | async-start | bytes 3932160 | tf_op jit(solution)/shard_map/reduce_scatter | solution.py:20
  67.7 1.8 %copy-start.2 = (bf16[1,1024,768]{2,1,0:T(8,128)(2,1)S(1)}, bf16[1,1024,768]{2,1,0:T(8,128)(2,1)}, u32[]{:S(2)}) copy-start(bf16[1,1024,768]{2,1,0:T(8,128)(2,1)} %param.15) | copy-start | bytes 4718596
  67.7 1.9 %copy-start.5 = (bf16[288,768]{1,0:T(8,128)(2,1)S(1)}, bf16[288,768]{1,0:T(8,128)(2,1)}, u32[]{:S(2)}) copy-start(bf16[288,768]{1,0:T(8,128)(2,1)} %all-reduce.2.cloned.1.call-done) | copy-start | bytes 1327108
  71.2 11.5 %all-to-all-start.1 = ((bf16[2,144,1024]{2,1,0:T(8,128)(2,1)}), bf16[2,144,1024]{2,1,0:T(8,128)(2,1)S(1)}, u32[]{:S(2)}, u32[]{:S(2)}) async-start(bf16[2,144,1024]{2,1,0:T(8,128)(2,1)} %bitcast.11), calls=%async_computation.1 | async-start | bytes 1179648 | tf_op jit(solution)/shard_map/all_to_all | solution.py:65
Sparse Core Ops, SparseCore 0:
  29.8 37.9 all-reduce.1
Sparse Core Ops, SparseCore 1:
  32.6 38.2 reduce-scatter.1
where the time goes:
time: 94.6 us; the launch traced here: 94.2 us
  waiting for transfers between devices  43.2 us (46%)
  between operations  15.6 us (16%)
  blocking collectives  12.8 us (14%)
  matrix products  7.69 us (8%)
  local copies, waits for them, and re-layouts  7.04 us (7%)
  other arithmetic  4.23 us (4%)
  starting transfers between devices  3.58 us (4%)
    psum x1, waiting for transfers between devices, body(): lax.psum(partial_value.astype(jnp.bfloat16), 'ec').astype(jnp.float32)  35.2 us
    all_to_all x1, blocking collectives, body(): lax.all_to_all(outgoing, 'er', split_axis=0, concat_axis=0, tiled=True)  12.8 us
    all_to_all x1, waiting for transfers between devices, body(): lax.all_to_all(slot_grad, 'er', split_axis=0, concat_axis=0, tiled=True)  7.97 us
    all_to_all x1, starting transfers between devices, body(): lax.all_to_all(slot_grad, 'er', split_axis=0, concat_axis=0, tiled=True)  3.5 us
    dot_general x1, matrix products, reduce_weights(): lax.dot_general(hidden, arrived, (((0,), (0,)), ((), ())), preferred_elem...  2.75 us
    broadcast_in_dim x1, other arithmetic, body(): return (input_grad[None], down_part[None])  2.1 us
    gather x1, local copies, waits for them, and re-layouts, body(): scaled[source]  2.07 us
    gather x1, local copies, waits for them, and re-layouts, body(): input_grad = returned[position]  1.96 us
  transfers between devices with their start and end apart: 3, of which 2 were waited for; matrix products, arithmetic and copies ran while one was open for 9% of the time, Pallas kernels for 0%

commit v1 on v0

v1 whole, which is shorter than its diff:
```python
import functools

import jax
import jax.numpy as jnp
from jax import lax
from jax.experimental import pallas as pl
from jax.experimental.pallas import tpu as pltpu
from jax.sharding import PartitionSpec as P


VMEM_LIMIT = 12 * 1024 * 1024


def shift(x, axis, step):
    n = lax.axis_size(axis)
    return lax.ppermute(x, axis, [(j, (j + step) % n) for j in range(n)])


def swap(x, axis, bit):
    return lax.ppermute(x, axis, [(j, j ^ bit) for j in range(lax.axis_size(axis))])


def wrap(x, n):
    return jnp.where(x < 0, x + n, x)


def matmul_nt(a, b):
    return lax.dot_general(a, b, (((1,), (1,)), ((), ())), preferred_element_type=jnp.float32)


def matmul_tn(a, b):
    return lax.dot_general(a, b, (((0,), (0,)), ((), ())), preferred_element_type=jnp.float32)


def call(kernel, outs, *args, stored=(), scratch=(), to_hbm=False, flops=1e6):
    vmem = pl.BlockSpec(memory_space=pltpu.VMEM)
    hbm = pl.BlockSpec(memory_space=pltpu.HBM)
    out_type = pltpu.HBM if to_hbm else pltpu.VMEM
    result = pl.pallas_call(
        kernel,
        out_shape=[out_type(shape, dtype) for shape, dtype in outs],
        in_specs=[vmem] * len(args) + [hbm] * len(stored),
        out_specs=[hbm if to_hbm else vmem] * len(outs),
        scratch_shapes=list(scratch),
        compiler_params=pltpu.CompilerParams(vmem_limit_bytes=VMEM_LIMIT),
        cost_estimate=pl.CostEstimate(flops=int(flops), transcendentals=0, bytes_accessed=1024),
    )(*args, *(pltpu.with_memory_space_constraint(x, pltpu.HBM) for x in stored))
    return result if len(outs) > 1 else result[0]


def load(sources, targets, sems):
    copies = [pltpu.make_async_copy(x, y, sems.at[i]) for i, (x, y) in enumerate(zip(sources, targets))]
    for copy in copies:
        copy.start()
    return copies


def half_index():
    me = lax.axis_index("ec")
    return lax.shift_right_logical(me + 1, 1) & 1


def one_hot(position, count):
    hit = lax.broadcasted_iota(jnp.int32, (count, position.shape[1]), 0) == position
    return hit, jnp.where(hit, 1.0, 0.0).astype(jnp.bfloat16)


def dispatch_kernel(ids, slots, probs, tokens, down, own, far, position, weights, v_ids, v_slots, v_probs, v_tokens, sems):
    capacity = own.shape[0]
    count = capacity + far.shape[0]
    copies = load((ids, slots, probs, tokens, down), (v_ids, v_slots, v_probs, v_tokens, weights), sems)
    for copy in copies[:4]:
        copy.wait()
    where = wrap(v_ids[...] - lax.axis_index("er"), count // capacity) * capacity + v_slots[...]
    position[...] = where
    hit, chosen = one_hot(where, count)
    prob = jnp.sum(jnp.where(hit, v_probs[...], 0.0), axis=1, keepdims=True)
    rows = lax.dot_general(chosen, v_tokens[...], (((1,), (0,)), ((), ())), preferred_element_type=jnp.float32)
    scaled = (prob * rows).astype(jnp.bfloat16)
    own[...] = scaled[:capacity]
    far[...] = scaled[capacity:]
    copies[4].wait()


def hidden_kernel(rows, weights, sent, kept):
    half = kept.shape[1]
    mine = half_index()
    value = rows[...]
    sent[...] = matmul_nt(value, weights[pl.ds(pl.multiple_of((1 - mine) * half, half), half), :]).astype(
        jnp.bfloat16
    )
    kept[...] = matmul_nt(value, weights[pl.ds(pl.multiple_of(mine * half, half), half), :])


def pair_kernel(kept, got, sent):
    sent[...] = (kept[...] + got[...].astype(jnp.float32)).astype(jnp.bfloat16)


def across_kernel(kept, got, more, total):
    total[...] = (kept[...] + got[...].astype(jnp.float32) + more[...].astype(jnp.float32)).astype(jnp.bfloat16)


def prepare_kernel(pre, up, gate, lift, hidden, by_gate, by_up, w_gate, w_up, v_pre, v_up, sems):
    copies = load((pre, up, gate, lift), (v_pre, v_up, w_gate, w_up), sems)
    for copy in copies[:2]:
        copy.wait()
    groups, capacity, _ = hidden.shape
    for step in range(groups):
        start = pl.multiple_of(wrap(lax.axis_index("er") - step, groups) * capacity, capacity)
        a = v_pre[pl.ds(start, capacity), :].astype(jnp.float32)
        u = v_up[pl.ds(start, capacity), :].astype(jnp.float32)
        s = jax.nn.sigmoid(a)
        hidden[step] = (a * s * u).astype(jnp.bfloat16)
        by_gate[step] = u * s * (1.0 + a * (1.0 - s))
        by_up[step] = a * s
    for copy in copies[2:]:
        copy.wait()


def grads_kernel(step, kept, other, by_gate, by_up, w_gate, w_up, out):
    half = kept.shape[1]
    mine = half_index()
    total = None
    for h in range(2):
        part = slice(h * half, (h + 1) * half)
        hid = jnp.where(mine == h, kept[...], other[...]).astype(jnp.float32)
        gate_grad = (hid * by_gate[step, :, part]).astype(jnp.bfloat16)
        up_grad = (hid * by_up[step, :, part]).astype(jnp.bfloat16)
        value = matmul_nt(gate_grad, w_gate[:, part]) + matmul_nt(up_grad, w_up[:, part])
        total = value if total is None else total + value
    out[...] = total.astype(jnp.bfloat16)


def weight_kernel(own, far, hidden, sent, kept):
    groups, capacity, _ = hidden.shape
    total = None
    for step in range(groups):
        rows = own[...] if step == 0 else far[(step - 1) * capacity : step * capacity]
        value = matmul_tn(hidden[step], rows)
        total = value if total is None else total + value
    pairs, block, _ = sent.shape
    for c in range(2):

        @pl.when((lax.axis_index("dp") & 1) == c)
        def _():
            for y in range(pairs):
                low, high = total[2 * y * block : (2 * y + 1) * block], total[(2 * y + 1) * block : (2 * y + 2) * block]
                kept[y] = high if c else low
                sent[y] = (low if c else high).astype(jnp.bfloat16)


def halve_kernel(bit, kept, got, sent, left):
    mine = lax.shift_right_logical(lax.axis_index("dp"), bit) & 1
    pairs = left.shape[0]
    for p in range(pairs):
        sent[p] = (kept[2 * p + 1 - mine] + got[2 * p + 1 - mine].astype(jnp.float32)).astype(jnp.bfloat16)
        left[p] = kept[2 * p + mine] + got[2 * p + mine].astype(jnp.float32)


def mean_kernel(replicas, kept, got, out, staged, sem):
    staged[...] = (kept[...] + got[...].astype(jnp.float32)) / replicas
    copy = pltpu.make_async_copy(staged, out, sem)
    copy.start()
    copy.wait()


def combine_kernel(pieces, position, own, back, out, staged, sems):
    capacity, count = own.shape[0], own.shape[0] + back.shape[0]
    _, chosen = one_hot(position[...], count)
    size = staged.shape[0] // pieces
    copies = []
    for i in range(pieces):
        part = slice(i * size, (i + 1) * size)
        value = matmul_tn(chosen[:capacity, part], own[...]) + matmul_tn(chosen[capacity:, part], back[...])
        staged[part] = value.astype(jnp.bfloat16)
        copies.append(pltpu.make_async_copy(staged.at[part], out.at[part], sems.at[i]))
        copies[-1].start()
    for copy in copies:
        copy.wait()


def start_sum(rows, weights):
    count, half = rows.shape[0], weights.shape[0] // 2
    flops = 4 * count * half * rows.shape[1]
    sent, kept = call(
        hidden_kernel, [((count, half), jnp.bfloat16), ((count, half), jnp.float32)], rows, weights, flops=flops
    )
    got = swap(sent, "ec", 1)
    sent = call(pair_kernel, [(sent.shape, jnp.bfloat16)], kept, got)
    more = swap(sent, "ec", 3)
    total = call(across_kernel, [(sent.shape, jnp.bfloat16)], kept, got, more)
    return total, swap(total, "ec", 1)


def fast_body(out_grad, route_probs, expert_ids, slot_ids, gate_pre, up_act, w_gate, w_up, w_down):
    tokens = out_grad[0]
    experts = lax.axis_size("er")
    replicas = lax.axis_size("dp")
    pre, up = gate_pre[0, 0], up_act[0, 0]
    capacity = pre.shape[0] // experts
    slot_count = experts * capacity
    count, width = tokens.shape
    hidden_size = pre.shape[1]
    bf16, f32, i32 = jnp.bfloat16, jnp.float32, jnp.int32
    own, far, position, down = call(
        dispatch_kernel,
        [
            ((capacity, width), bf16),
            ((slot_count - capacity, width), bf16),
            ((1, count), i32),
            ((hidden_size, width), bf16),
        ],
        stored=(expert_ids, slot_ids, route_probs, tokens, w_down[0]),
        scratch=[
            pltpu.VMEM((1, count), i32),
            pltpu.VMEM((1, count), i32),
            pltpu.VMEM((1, count), f32),
            pltpu.VMEM((count, width), bf16),
            pltpu.SemaphoreType.DMA((5,)),
        ],
        flops=2 * slot_count * tokens.size,
    )
    far = [shift(far[(s - 1) * capacity : s * capacity], "er", s) for s in range(1, experts)]
    rows = (experts, capacity, hidden_size)
    hidden, by_gate, by_up, gate, lift = call(
        prepare_kernel,
        [(rows, bf16), (rows, f32), (rows, f32), ((width, hidden_size), bf16), ((width, hidden_size), bf16)],
        stored=(pre, up, w_gate[0], w_up[0]),
        scratch=[pltpu.VMEM(pre.shape, bf16), pltpu.VMEM(pre.shape, bf16), pltpu.SemaphoreType.DMA((4,))],
        flops=1e9,
    )
    own_sum = start_sum(own, down)
    far_sums = [start_sum(x, down) for x in far]

    block = hidden_size // replicas
    sent, kept = call(
        weight_kernel,
        [((replicas // 2, block, width), bf16), ((replicas // 2, block, width), f32)],
        own,
        jnp.concatenate(far, 0) if len(far) > 1 else far[0],
        hidden,
        flops=2 * slot_count * hidden_size * width,
    )
    bit = 0
    while True:
        got = swap(sent, "dp", 1 << bit)
        if kept.shape[0] == 1:
            break
        bit += 1
        shape = (kept.shape[0] // 2, block, width)
        sent, kept = call(functools.partial(halve_kernel, bit), [(shape, bf16), (shape, f32)], kept, got, flops=1e8)
    down_part = call(
        functools.partial(mean_kernel, replicas),
        [(kept.shape, f32)],
        kept,
        got,
        scratch=[pltpu.VMEM(kept.shape, f32), pltpu.SemaphoreType.DMA],
        to_hbm=True,
    )

    def slot_grads(total, step):
        flops = 4 * capacity * hidden_size * width
        kernel = functools.partial(grads_kernel, step)
        return call(kernel, [((capacity, width), bf16)], *total, by_gate, by_up, gate, lift, flops=flops)

    grad_own = slot_grads(own_sum, 0)
    back = [shift(slot_grads(far_sums[s - 1], s), "er", -s) for s in range(1, experts)]
    pieces = 4 if count % 64 == 0 else 1
    input_grad = call(
        functools.partial(combine_kernel, pieces),
        [((count, width), bf16)],
        position,
        grad_own,
        jnp.concatenate(back, 0) if len(back) > 1 else back[0],
        scratch=[pltpu.VMEM((count, width), bf16), pltpu.SemaphoreType.DMA((pieces,))],
        to_hbm=True,
        flops=2 * slot_count * tokens.size,
    )
    return (input_grad[None], down_part)


def solution(mesh):
    in_specs = (
        P("dp", "er", "ec"),
        P("dp", "er"),
        P("dp", "er"),
        P("dp", "er"),
        P("dp", "er", None, None),
        P("dp", "er", None, None),
        P("er", "ec", None),
        P("er", "ec", None),
        P("er", None, "ec"),
    )
    out_specs = (P("dp", "er", "ec"), P("er", "dp", "ec"))
    return jax.shard_map(fast_body, mesh=mesh, in_specs=in_specs, out_specs=out_specs, check_vma=False)
```

time: 94.6 us -> 51.2 us (0.54)
  waiting for transfers between devices: 43.2 us -> 21.9 us
  between operations: 15.6 us -> 0.75 us
  starting transfers between devices: 3.58 us -> 17.1 us
  blocking collectives: 12.8 us -> 0 us
  Pallas kernels: 0 us -> 11.2 us
  matrix products: 7.69 us -> 0 us
  local copies, waits for them, and re-layouts: 7.04 us -> 0 us
  other arithmetic: 4.23 us -> 0 us
    psum x1 -> x0, waiting for transfers between devices: 35.2 us -> none  [body(): lax.psum(partial_value.astype(jnp.bfloat16), 'ec').astype(jnp.float32)]
    ppermute x0 -> x10, waiting for transfers between devices: none -> 21.9 us  [the longest x8 17.1 us: swap(): lax.ppermute(x, axis, [(j, j ^ bit) for j in range(lax.axis_size(axis))])]
    ppermute x0 -> x10, starting transfers between devices: none -> 17.1 us  [the longest x8 12.5 us: swap(): lax.ppermute(x, axis, [(j, j ^ bit) for j in range(lax.axis_size(axis))])]
    all_to_all x1 -> x0, blocking collectives: 12.8 us -> none  [body(): lax.all_to_all(outgoing, 'er', split_axis=0, concat_axis=0, tiled=True)]
    pallas_call x0 -> x14, Pallas kernels: none -> 11.2 us  [call(): pl.pallas_call(kernel, out_shape=[out_type(shape, dtype) for shape, dtype...]
    all_to_all x1 -> x0, waiting for transfers between devices: 7.97 us -> none  [body(): lax.all_to_all(slot_grad, 'er', split_axis=0, concat_axis=0, tiled=True)]
    dot_general x4 -> x0, matrix products: 7.69 us -> none  [the longest x1 2.75 us: reduce_weights(): lax.dot_general(hidden, arrived, (((0,), (0,)), ((), ())), preferred_elem...]
    gather x2 -> x0, local copies, waits for them, and re-layouts: 4.03 us -> none  [the longest x1 2.07 us: body(): scaled[source]]
  transfers between devices with their start and end apart: 3 -> 10, of which waited for: 2 -> 7; matrix products, arithmetic and copies ran while one was open for 9% -> 0% of each run, Pallas kernels for 0% -> 14%
where the time goes in v1:
time: 51.2 us; the launch traced here: 51 us
  waiting for transfers between devices  21.9 us (43%)
  starting transfers between devices  17.1 us (33%)
  Pallas kernels  11.2 us (22%)
  between operations  0.75 us (1%)
    ppermute x8, waiting for transfers between devices, swap(): lax.ppermute(x, axis, [(j, j ^ bit) for j in range(lax.axis_size(axis))])  17.1 us
    ppermute x8, starting transfers between devices, swap(): lax.ppermute(x, axis, [(j, j ^ bit) for j in range(lax.axis_size(axis))])  12.5 us
    pallas_call x14, Pallas kernels, call(): pl.pallas_call(kernel, out_shape=[out_type(shape, dtype) for shape, dtype...  11.2 us
    ppermute x2, waiting for transfers between devices, shift(): return lax.ppermute(x, axis, [(j, (j + step) % n) for j in range(n)])  4.81 us
    ppermute x2, starting transfers between devices, shift(): return lax.ppermute(x, axis, [(j, (j + step) % n) for j in range(n)])  4.57 us
  transfers between devices with their start and end apart: 10, of which 7 were waited for; matrix products, arithmetic and copies ran while one was open for 0% of the time, Pallas kernels for 14%

profile of v1, /device:TPU:0, one launch (start us, length us, event | category | flops | bytes accessed | tf_op | source)
XLA Modules:
  0.0 51.0 jit_solution(17629287510985845699)
XLA Ops:
  0.6 1.7 %shard_map.104 = (bf16[144,1024]{1,0:T(8,128)(2,1)S(1)}, bf16[144,1024]{1,0:T(8,128)(2,1)S(1)}, s32[1,256]{1,0:T(1,128)S(1)}, bf16[768,1024]{1,0:T(8,128)(2,1)S(1)}) custom-call(s32[1,256]{1,0:T(1,128)} %ids.1, s32[1,256]{1,0:T(1,128)} %slots.1, f32[1,256]{1,0:T(1,128)} %probs.1, bf16[256,1024]{1,0:T(8,128)(2,1)} %bitcast.10, bf16[768,1024]{1,0:T(8,128)(2,1)} %bitcast.7), custom_call_target="tpu_custom_call" | custom-call | flops 150994944 | bytes 1024 | tf_op jit(solution)/shard_map/pallas_call | solution.py:39
  2.3 3.0 %collective-permute-start.3 = (bf16[144,1024]{1,0:T(8,128)(2,1)S(1)}, bf16[144,1024]{1,0:T(8,128)(2,1)S(1)}, u32[]{:S(2)}, u32[]{:S(2)}) collective-permute-start(bf16[144,1024]{1,0:T(8,128)(2,1)S(1)} %get-tuple-element.28), channel_id=1, source_target_pairs={{0,16},{16,0},{1,17},{17,1},{2,18},{18,2},{3,19},{19,3},{4,20},{20... | collective-permute-start | bytes 884744 | tf_op jit(solution)/shard_map/ppermute | solution.py:16
  5.3 2.2 %shard_map.108 = (bf16[2,144,768]{2,1,0:T(8,128)(2,1)S(1)}, f32[2,144,768]{2,1,0:T(8,128)S(1)}, f32[2,144,768]{2,1,0:T(8,128)S(1)}, bf16[1024,768]{1,0:T(8,128)(2,1)S(1)}, bf16[1024,768]{1,0:T(8,128)(2,1)S(1)}) custom-call(bf16[288,768]{1,0:T(8,128)(2,1)} %bitcast.12, bf16[288,768]{1,0:T(8,128)(2,1)} %bitcast.13, bf16[1024,768]{1,0:T(8,128)(2,1)} %bitcast.8, ...), custom_call_target="tpu_custom_call" | custom-call | flops 1000000000 | bytes 1024 | tf_op jit(solution)/shard_map/pallas_call | solution.py:39
  7.5 4.8 %collective-permute-done.3.rows.far = bf16[144,1024]{1,0:T(8,128)(2,1)S(1)} collective-permute-done((bf16[144,1024]{1,0:T(8,128)(2,1)S(1)}, bf16[144,1024]{1,0:T(8,128)(2,1)S(1)}, u32[]{:S(2)}, u32[]{:S(2)}) %collective-permute-start.3) | collective-permute-done | bytes 294944 | tf_op jit(solution)/shard_map/ppermute | solution.py:16
  12.3 1.2 %shard_map.115 = (bf16[2,192,1024]{2,1,0:T(8,128)(2,1)S(1)}, f32[2,192,1024]{2,1,0:T(8,128)S(1)}) custom-call(bf16[144,1024]{1,0:T(8,128)(2,1)S(1)} %get-tuple-element.20.rows.own, bf16[144,1024]{1,0:T(8,128)(2,1)S(1)} %collective-permute-done.3.rows.far, bf16[2,144,768]{2,1,0:T(8,128)(2,1)S(1)} %get-tuple-element.31.hidden), custom_call_target="tpu_custom_call" | custom-call | flops 452984832 | bytes 1024 | tf_op jit(solution)/shard_map/pallas_call | solution.py:39
  13.5 0.1 collective-permute-start.8
  13.6 0.6 %shard_map.110 = (bf16[144,384]{1,0:T(8,128)(2,1)S(1)}, f32[144,384]{1,0:T(8,128)S(1)}) custom-call(bf16[144,1024]{1,0:T(8,128)(2,1)S(1)} %collective-permute-done.3.rows.far, bf16[768,1024]{1,0:T(8,128)(2,1)S(1)} %get-tuple-element.21.weights), custom_call_target="tpu_custom_call" | custom-call | flops 226492416 | bytes 1024 | tf_op jit(solution)/shard_map/pallas_call | solution.py:39
  14.2 1.9 %collective-permute-start.4 = (bf16[144,384]{1,0:T(8,128)(2,1)S(1)}, bf16[144,384]{1,0:T(8,128)(2,1)S(1)}, u32[]{:S(2)}, u32[]{:S(2)}) collective-permute-start(bf16[144,384]{1,0:T(8,128)(2,1)S(1)} %get-tuple-element.30), channel_id=1, source_target_pairs={{0,4},{4,0},{8,12},{12,8},{1,5},{5,1},{9,13},{13,9},{2,6},{6,2},{1... | collective-permute-start | bytes 331784 | tf_op jit(solution)/shard_map/ppermute | solution.py:20
  16.1 3.7 %collective-permute-done.4.got = bf16[144,384]{1,0:T(8,128)(2,1)S(1)} collective-permute-done((bf16[144,384]{1,0:T(8,128)(2,1)S(1)}, bf16[144,384]{1,0:T(8,128)(2,1)S(1)}, u32[]{:S(2)}, u32[]{:S(2)}) %collective-permute-start.4) | collective-permute-done | bytes 110624 | tf_op jit(solution)/shard_map/ppermute | solution.py:20
  19.8 3.8 %collective-permute-start.5 = (bf16[144,384]{1,0:T(8,128)(2,1)S(1)}, bf16[144,384]{1,0:T(8,128)(2,1)S(1)}, u32[]{:S(2)}, u32[]{:S(2)}) collective-permute-start(bf16[144,384]{1,0:T(8,128)(2,1)S(1)} %shard_map.111), channel_id=1, source_target_pairs={{0,12},{4,8},{8,4},{12,0},{1,13},{5,9},{9,5},{13,1},{2,14},{6,10},... | collective-permute-start | bytes 331784 | tf_op jit(solution)/shard_map/ppermute | solution.py:20
  23.7 3.0 %collective-permute-done.5.more = bf16[144,384]{1,0:T(8,128)(2,1)S(1)} collective-permute-done((bf16[144,384]{1,0:T(8,128)(2,1)S(1)}, bf16[144,384]{1,0:T(8,128)(2,1)S(1)}, u32[]{:S(2)}, u32[]{:S(2)}) %collective-permute-start.5) | collective-permute-done | bytes 110624 | tf_op jit(solution)/shard_map/ppermute | solution.py:20
  26.7 2.0 %collective-permute-start.6 = (bf16[144,384]{1,0:T(8,128)(2,1)S(1)}, bf16[144,384]{1,0:T(8,128)(2,1)S(1)}, u32[]{:S(2)}, u32[]{:S(2)}) collective-permute-start(bf16[144,384]{1,0:T(8,128)(2,1)S(1)} %shard_map.112.kept), channel_id=1, source_target_pairs={{0,4},{4,0},{8,12},{12,8},{1,5},{5,1},{9,13},{13,9},{2,6},{6,2},{1... | collective-permute-start | bytes 331784 | tf_op jit(solution)/shard_map/ppermute | solution.py:20
  28.7 0.0 collective-permute-done.8.got
  28.7 0.2 shard_map.116
  28.9 1.6 %collective-permute-start.9 = (bf16[1,192,1024]{2,1,0:T(8,128)(2,1)S(1)}, bf16[1,192,1024]{2,1,0:T(8,128)(2,1)S(1)}, u32[]{:S(2)}, u32[]{:S(2)}) collective-permute-start(bf16[1,192,1024]{2,1,0:T(8,128)(2,1)S(1)} %get-tuple-element.35), channel_id=1, source_target_pairs={{0,2},{1,3},{2,0},{3,1},{4,6},{5,7},{6,4},{7,5},{8,10},{9,11},{10,... | collective-permute-start | bytes 1179656 | tf_op jit(solution)/shard_map/ppermute | solution.py:20
  30.5 0.6 %shard_map.105 = (bf16[144,384]{1,0:T(8,128)(2,1)S(1)}, f32[144,384]{1,0:T(8,128)S(1)}) custom-call(bf16[144,1024]{1,0:T(8,128)(2,1)S(1)} %get-tuple-element.20.rows.own, bf16[768,1024]{1,0:T(8,128)(2,1)S(1)} %get-tuple-element.21.weights), custom_call_target="tpu_custom_call" | custom-call | flops 226492416 | bytes 1024 | tf_op jit(solution)/shard_map/pallas_call | solution.py:39
  31.1 0.1 collective-permute-start
  31.2 0.6 %collective-permute-done.6.other = bf16[144,384]{1,0:T(8,128)(2,1)S(1)} collective-permute-done((bf16[144,384]{1,0:T(8,128)(2,1)S(1)}, bf16[144,384]{1,0:T(8,128)(2,1)S(1)}, u32[]{:S(2)}, u32[]{:S(2)}) %collective-permute-start.6) | collective-permute-done | bytes 110624 | tf_op jit(solution)/shard_map/ppermute | solution.py:20
  31.8 1.2 %shard_map.113 = bf16[144,1024]{1,0:T(8,128)(2,1)S(1)} custom-call(bf16[144,384]{1,0:T(8,128)(2,1)S(1)} %shard_map.112.kept, bf16[144,384]{1,0:T(8,128)(2,1)S(1)} %collective-permute-done.6.other, f32[2,144,768]{2,1,0:T(8,128)S(1)} %get-tuple-element.24.by_gate, f32[2,144,768]{2,1,0:T(8,128)S(1)} %get-tuple-element.25.by_up, ...), custom_call_target="tpu_custom_call" | custom-call | flops 452984832 | bytes 1024 | tf_op jit(solution)/shard_map/pallas_call | solution.py:39
  33.0 1.5 %collective-permute-start.7 = (bf16[144,1024]{1,0:T(8,128)(2,1)S(1)}, bf16[144,1024]{1,0:T(8,128)(2,1)S(1)}, u32[]{:S(2)}, u32[]{:S(2)}) collective-permute-start(bf16[144,1024]{1,0:T(8,128)(2,1)S(1)} %shard_map.113), channel_id=1, source_target_pairs={{0,16},{16,0},{1,17},{17,1},{2,18},{18,2},{3,19},{19,3},{4,20},{20... | collective-permute-start | bytes 884744 | tf_op jit(solution)/shard_map/ppermute | solution.py:16
  34.5 1.4 %collective-permute-done.got = bf16[144,384]{1,0:T(8,128)(2,1)S(1)} collective-permute-done((bf16[144,384]{1,0:T(8,128)(2,1)S(1)}, bf16[144,384]{1,0:T(8,128)(2,1)S(1)}, u32[]{:S(2)}, u32[]{:S(2)}) %collective-permute-start) | collective-permute-done | bytes 110624 | tf_op jit(solution)/shard_map/ppermute | solution.py:20
  35.9 2.9 %collective-permute-start.1 = (bf16[144,384]{1,0:T(8,128)(2,1)S(1)}, bf16[144,384]{1,0:T(8,128)(2,1)S(1)}, u32[]{:S(2)}, u32[]{:S(2)}) collective-permute-start(bf16[144,384]{1,0:T(8,128)(2,1)S(1)} %shard_map.106), channel_id=1, source_target_pairs={{0,12},{4,8},{8,4},{12,0},{1,13},{5,9},{9,5},{13,1},{2,14},{6,10},... | collective-permute-start | bytes 331784 | tf_op jit(solution)/shard_map/ppermute | solution.py:20
  38.9 3.7 %collective-permute-done.1.more = bf16[144,384]{1,0:T(8,128)(2,1)S(1)} collective-permute-done((bf16[144,384]{1,0:T(8,128)(2,1)S(1)}, bf16[144,384]{1,0:T(8,128)(2,1)S(1)}, u32[]{:S(2)}, u32[]{:S(2)}) %collective-permute-start.1) | collective-permute-done | bytes 110624 | tf_op jit(solution)/shard_map/ppermute | solution.py:20
  42.7 0.1 collective-permute-start.2
  42.7 4.7 %collective-permute-done.2.other = bf16[144,384]{1,0:T(8,128)(2,1)S(1)} collective-permute-done((bf16[144,384]{1,0:T(8,128)(2,1)S(1)}, bf16[144,384]{1,0:T(8,128)(2,1)S(1)}, u32[]{:S(2)}, u32[]{:S(2)}) %collective-permute-start.2) | collective-permute-done | bytes 110624 | tf_op jit(solution)/shard_map/ppermute | solution.py:20
  47.5 1.2 %shard_map.109.own = bf16[144,1024]{1,0:T(8,128)(2,1)S(1)} custom-call(bf16[144,384]{1,0:T(8,128)(2,1)S(1)} %shard_map.107.kept, bf16[144,384]{1,0:T(8,128)(2,1)S(1)} %collective-permute-done.2.other, f32[2,144,768]{2,1,0:T(8,128)S(1)} %get-tuple-element.24.by_gate, f32[2,144,768]{2,1,0:T(8,128)S(1)} %get-tuple-element.25.by_up, ...), custom_call_target="tpu_custom_call" | custom-call | flops 452984832 | bytes 1024 | tf_op jit(solution)/shard_map/pallas_call | solution.py:39
  48.6 0.0 collective-permute-done.7.back
  48.7 1.3 %shard_map.114 = bf16[256,1024]{1,0:T(8,128)(2,1)} custom-call(s32[1,256]{1,0:T(1,128)S(1)} %get-tuple-element.19.position, bf16[144,1024]{1,0:T(8,128)(2,1)S(1)} %shard_map.109.own, bf16[144,1024]{1,0:T(8,128)(2,1)S(1)} %collective-permute-done.7.back), custom_call_target="tpu_custom_call" | custom-call | flops 150994944 | bytes 1024 | tf_op jit(solution)/shard_map/pallas_call | solution.py:39
  50.0 0.0 collective-permute-done.9.got
  50.0 1.0 %shard_map.117 = f32[1,192,1024]{2,1,0:T(8,128)} custom-call(f32[1,192,1024]{2,1,0:T(8,128)S(1)} %get-tuple-element.34.kept, bf16[1,192,1024]{2,1,0:T(8,128)(2,1)S(1)} %collective-permute-done.9.got), custom_call_target="tpu_custom_call" | custom-call | flops 1000000 | bytes 1024 | tf_op jit(solution)/shard_map/pallas_call | solution.py:39
  (4 shorter events, 0.1 us)
Async XLA Ops:
  2.3 10.0 %collective-permute-start.3 = (bf16[144,1024]{1,0:T(8,128)(2,1)S(1)}, bf16[144,1024]{1,0:T(8,128)(2,1)S(1)}, u32[]{:S(2)}, u32[]{:S(2)}) collective-permute-start(bf16[144,1024]{1,0:T(8,128)(2,1)S(1)} %get-tuple-element.28), channel_id=1, source_target_pairs={{0,16},{16,0},{1,17},{17,1},{2,18},{18,2},{3,19},{19,3},{4,20},{20... | collective-permute-start | bytes 884744 | tf_op jit(solution)/shard_map/ppermute | solution.py:16
  13.5 15.2 %collective-permute-start.8 = (bf16[2,192,1024]{2,1,0:T(8,128)(2,1)S(1)}, bf16[2,192,1024]{2,1,0:T(8,128)(2,1)S(1)}, u32[]{:S(2)}, u32[]{:S(2)}) collective-permute-start(bf16[2,192,1024]{2,1,0:T(8,128)(2,1)S(1)} %get-tuple-element.33), channel_id=1, source_target_pairs={{0,1},{1,0},{2,3},{3,2},{4,5},{5,4},{6,7},{7,6},{8,9},{9,8},{10,11... | collective-permute-start | bytes 2359304 | tf_op jit(solution)/shard_map/ppermute | solution.py:20
  14.2 5.6 %collective-permute-start.4 = (bf16[144,384]{1,0:T(8,128)(2,1)S(1)}, bf16[144,384]{1,0:T(8,128)(2,1)S(1)}, u32[]{:S(2)}, u32[]{:S(2)}) collective-permute-start(bf16[144,384]{1,0:T(8,128)(2,1)S(1)} %get-tuple-element.30), channel_id=1, source_target_pairs={{0,4},{4,0},{8,12},{12,8},{1,5},{5,1},{9,13},{13,9},{2,6},{6,2},{1... | collective-permute-start | bytes 331784 | tf_op jit(solution)/shard_map/ppermute | solution.py:20
  19.8 6.8 %collective-permute-start.5 = (bf16[144,384]{1,0:T(8,128)(2,1)S(1)}, bf16[144,384]{1,0:T(8,128)(2,1)S(1)}, u32[]{:S(2)}, u32[]{:S(2)}) collective-permute-start(bf16[144,384]{1,0:T(8,128)(2,1)S(1)} %shard_map.111), channel_id=1, source_target_pairs={{0,12},{4,8},{8,4},{12,0},{1,13},{5,9},{9,5},{13,1},{2,14},{6,10},... | collective-permute-start | bytes 331784 | tf_op jit(solution)/shard_map/ppermute | solution.py:20
  26.7 5.1 %collective-permute-start.6 = (bf16[144,384]{1,0:T(8,128)(2,1)S(1)}, bf16[144,384]{1,0:T(8,128)(2,1)S(1)}, u32[]{:S(2)}, u32[]{:S(2)}) collective-permute-start(bf16[144,384]{1,0:T(8,128)(2,1)S(1)} %shard_map.112.kept), channel_id=1, source_target_pairs={{0,4},{4,0},{8,12},{12,8},{1,5},{5,1},{9,13},{13,9},{2,6},{6,2},{1... | collective-permute-start | bytes 331784 | tf_op jit(solution)/shard_map/ppermute | solution.py:20
  28.9 21.1 %collective-permute-start.9 = (bf16[1,192,1024]{2,1,0:T(8,128)(2,1)S(1)}, bf16[1,192,1024]{2,1,0:T(8,128)(2,1)S(1)}, u32[]{:S(2)}, u32[]{:S(2)}) collective-permute-start(bf16[1,192,1024]{2,1,0:T(8,128)(2,1)S(1)} %get-tuple-element.35), channel_id=1, source_target_pairs={{0,2},{1,3},{2,0},{3,1},{4,6},{5,7},{6,4},{7,5},{8,10},{9,11},{10,... | collective-permute-start | bytes 1179656 | tf_op jit(solution)/shard_map/ppermute | solution.py:20
  31.1 4.8 %collective-permute-start = (bf16[144,384]{1,0:T(8,128)(2,1)S(1)}, bf16[144,384]{1,0:T(8,128)(2,1)S(1)}, u32[]{:S(2)}, u32[]{:S(2)}) collective-permute-start(bf16[144,384]{1,0:T(8,128)(2,1)S(1)} %get-tuple-element.23), channel_id=1, source_target_pairs={{0,4},{4,0},{8,12},{12,8},{1,5},{5,1},{9,13},{13,9},{2,6},{6,2},{1... | collective-permute-start | bytes 331784 | tf_op jit(solution)/shard_map/ppermute | solution.py:20
  33.0 15.7 %collective-permute-start.7 = (bf16[144,1024]{1,0:T(8,128)(2,1)S(1)}, bf16[144,1024]{1,0:T(8,128)(2,1)S(1)}, u32[]{:S(2)}, u32[]{:S(2)}) collective-permute-start(bf16[144,1024]{1,0:T(8,128)(2,1)S(1)} %shard_map.113), channel_id=1, source_target_pairs={{0,16},{16,0},{1,17},{17,1},{2,18},{18,2},{3,19},{19,3},{4,20},{20... | collective-permute-start | bytes 884744 | tf_op jit(solution)/shard_map/ppermute | solution.py:16
  35.9 6.7 %collective-permute-start.1 = (bf16[144,384]{1,0:T(8,128)(2,1)S(1)}, bf16[144,384]{1,0:T(8,128)(2,1)S(1)}, u32[]{:S(2)}, u32[]{:S(2)}) collective-permute-start(bf16[144,384]{1,0:T(8,128)(2,1)S(1)} %shard_map.106), channel_id=1, source_target_pairs={{0,12},{4,8},{8,4},{12,0},{1,13},{5,9},{9,5},{13,1},{2,14},{6,10},... | collective-permute-start | bytes 331784 | tf_op jit(solution)/shard_map/ppermute | solution.py:20
  42.7 4.8 %collective-permute-start.2 = (bf16[144,384]{1,0:T(8,128)(2,1)S(1)}, bf16[144,384]{1,0:T(8,128)(2,1)S(1)}, u32[]{:S(2)}, u32[]{:S(2)}) collective-permute-start(bf16[144,384]{1,0:T(8,128)(2,1)S(1)} %shard_map.107.kept), channel_id=1, source_target_pairs={{0,4},{4,0},{8,12},{12,8},{1,5},{5,1},{9,13},{13,9},{2,6},{6,2},{1... | collective-permute-start | bytes 331784 | tf_op jit(solution)/shard_map/ppermute | solution.py:20
